TPU v7x, 32 devices: a whole 2x2x4 slice. The times are simulated.
32 devices in a mesh: seq: 8 (over z, y), ch: 4 (over x, core).
Axes of the slice: x: 2, y: 2, z: 4, core: 2. Of those that a mesh axis runs over, the one named last changes fastest.
Arguments:
- inputs: bfloat16 [8192, 768], P(('seq', 'ch')), may hold values from -6 to 6
- gain_one: float32 [768], replicated, may hold values from 0.5 to 1.5
- shift_one: float32 [768], replicated, may hold values from -1.5 to 1.5
- conv_weight: bfloat16 [3, 768, 384], P(None, None, 'ch'), may hold values from -0.125 to 0.125
- gain_two: float32 [384], P('ch'), may hold values from 0.5 to 1.5
- shift_two: float32 [384], P('ch'), may hold values from -1.5 to 1.5
- mix_weight: bfloat16 [384, 768], P('ch'), may hold values from -0.3125 to 0.3125
- head_weight: bfloat16 [768, 6956], P('ch'), may hold values from -0.21875 to 0.21875
- head_bias: float32 [6956], replicated, may hold values from -2 to 2
- species: int32 [8], replicated, may hold values from 0 to 1, as said below
- counts: int32 [8192, 5313], P(('seq', 'ch')), may hold values from 0 to 3
Outputs:
- outputs: bfloat16 [8192, 768], P(('seq', 'ch'))
- input_grad: float32 [8192, 768], P(('seq', 'ch'))
- gain_one_grad: float32 [768], replicated
- shift_one_grad: float32 [768], replicated
- conv_weight_grad: float32 [3, 768, 384], P(None, None, 'ch')
- gain_two_grad: float32 [384], P('ch')
- shift_two_grad: float32 [384], P('ch')
- mix_weight_grad: float32 [384, 768], P('ch')
- head_weight_grad: float32 [768, 6956], P(('seq', 'ch'))
- head_bias_grad: float32 [6956], replicated
Inputs may be any that keep to these rules, and one draw needn't show every extreme that they name: Each window holds one species, given by species[w]; both species occur in every draw.
All inputs are finite; a program needn't handle non-finite values.
Results may differ from a plain program's by a relative error of at most 0.014.
Values may be sent and summed in bfloat16 or wider, within the bound.
A program may use at most 192 MiB of HBM per device.

v0:
```python
import jax
import jax.numpy as jnp
from jax import lax
from jax.sharding import PartitionSpec as P

HUMAN = 5313
MOUSE = 1643
DILATION_STEP = 11
TAPS = 3
WINDOW_BINS = 1024
SHIFT = 512
norm_eps = 1e-05
contract_rows = (((0,), (0,)), ((), ()))
contract_cols = (((1,), (1,)), ((), ()))


def with_halo(cells, sides, width):
    for axis, dim in sides:
        count = lax.axis_size(axis)
        head = lax.slice_in_dim(cells, 0, width, axis=dim)
        tail = lax.slice_in_dim(cells, cells.shape[dim] - width, cells.shape[dim], axis=dim)
        cells = jnp.concatenate(
            [
                lax.ppermute(tail, axis, [(i, (i + 1) % count) for i in range(count)]),
                cells,
                lax.ppermute(head, axis, [((i + 1) % count, i) for i in range(count)]),
            ],
            axis=dim,
        )
    return cells


def window_lookup(position, total_bins):
    return jnp.mod(position - SHIFT, total_bins) // WINDOW_BINS


def gelu_grad(value, upstream):
    _, pullback = jax.vjp(jax.nn.gelu, value)
    return pullback(upstream)[0]


def poisson_grad(logits, target):
    rate = jax.nn.softplus(logits)
    return (jax.nn.sigmoid(logits) * (1.0 - target / rate)).astype(jnp.bfloat16)


def on_device(
    inputs,
    gain_one,
    shift_one,
    conv_weight,
    gain_two,
    shift_two,
    mix_weight,
    head_weight,
    head_bias,
    species,
    counts,
):
    seq_count = lax.axis_size("seq")
    ch_count = lax.axis_size("ch")
    seq_index = lax.axis_index("seq")
    ch_index = lax.axis_index("ch")
    local_rows = inputs.shape[0]
    width = inputs.shape[1]
    conv_cols = conv_weight.shape[2]
    residual_rows = local_rows * ch_count
    every_bin_list = residual_rows * seq_count
    inv_bins = 1.0 / every_bin_list
    input_f = inputs.astype(jnp.float32)
    sum_one, square_one = lax.psum(
        (jnp.sum(input_f, 0), jnp.sum(input_f * input_f, 0)), ("seq", "ch")
    )
    mean_one = sum_one * inv_bins
    scale_one = lax.rsqrt(square_one * inv_bins - mean_one * mean_one + norm_eps)
    normed_one = (input_f - mean_one) * scale_one
    pre_one = normed_one * gain_one + shift_one
    act_one = jax.nn.gelu(pre_one).astype(jnp.bfloat16)
    residual_block = lax.all_gather(act_one, "ch", axis=0, tiled=True)
    padded_input = with_halo(residual_block, (("seq", 0),), DILATION_STEP)
    bin_positions = seq_index * residual_rows + jnp.arange(residual_rows, dtype=jnp.int32)
    local_window = window_lookup(bin_positions, every_bin_list)
    fwd_masks = [
        window_lookup(bin_positions + (kernel_tap_index - 1) * DILATION_STEP, every_bin_list)
        == local_window
        for kernel_tap_index in range(TAPS)
    ]
    back_masks = [
        (
            window_lookup(bin_positions - (kernel_tap_index - 1) * DILATION_STEP, every_bin_list)
            == local_window
        ).astype(jnp.float32)[:, None]
        for kernel_tap_index in range(TAPS)
    ]
    conv_out = jnp.zeros((residual_rows, conv_cols), jnp.float32)
    for kernel_tap_index in range(TAPS):
        product = jnp.dot(
            padded_input[
                kernel_tap_index * DILATION_STEP : kernel_tap_index * DILATION_STEP + residual_rows
            ],
            conv_weight[kernel_tap_index],
            preferred_element_type=jnp.float32,
        )
        conv_out = conv_out + jnp.where(fwd_masks[kernel_tap_index][:, None], product, 0.0)
    sum_two, square_two = lax.psum((jnp.sum(conv_out, 0), jnp.sum(conv_out * conv_out, 0)), "seq")
    mean_two = sum_two * inv_bins
    scale_two = lax.rsqrt(square_two * inv_bins - mean_two * mean_two + norm_eps)
    normed_two = (conv_out - mean_two) * scale_two
    pre_two = normed_two * gain_two + shift_two
    act_two = jax.nn.gelu(pre_two).astype(jnp.bfloat16)
    branch = lax.psum_scatter(
        jnp.dot(act_two, mix_weight, preferred_element_type=jnp.float32).astype(jnp.bfloat16),
        "ch",
        scatter_dimension=0,
        tiled=True,
    ).astype(jnp.float32)
    outputs = (input_f + branch).astype(jnp.bfloat16)
    row_start = seq_index * residual_rows + ch_index * local_rows
    window_index = window_lookup(row_start, every_bin_list)
    window_ids = jnp.arange(species.shape[0], dtype=jnp.int32)
    my_species = jnp.sum(jnp.where(window_ids == window_index, species, 0))
    is_human = my_species == 0
    targets = counts.astype(jnp.float32)
    zero_human = jnp.zeros((local_rows, HUMAN), jnp.bfloat16)
    zero_mouse = jnp.zeros((local_rows, MOUSE), jnp.bfloat16)
    start_logits = (
        jnp.zeros((local_rows, HUMAN), jnp.float32),
        jnp.zeros((local_rows, MOUSE), jnp.float32),
    )
    piece = lax.all_gather(head_weight, "ch", axis=0, tiled=True)

    def human_add(unused):
        return (
            jnp.dot(outputs, piece[:, :HUMAN], preferred_element_type=jnp.float32),
            start_logits[1],
        )

    def mouse_add(unused):
        return (
            start_logits[0],
            jnp.dot(outputs, piece[:, HUMAN:], preferred_element_type=jnp.float32),
        )

    logit_sums = lax.cond(is_human, human_add, mouse_add, 0)

    def human_grads(unused):
        return (poisson_grad(logit_sums[0] + head_bias[:HUMAN], targets), zero_mouse)

    def mouse_grads(unused):
        return (zero_human, poisson_grad(logit_sums[1] + head_bias[HUMAN:], targets[:, :MOUSE]))

    grad_human, grad_mouse = lax.cond(is_human, human_grads, mouse_grads, 0)

    def back_piece(piece):

        def human_back(unused):
            return lax.dot_general(
                grad_human, piece[:, :HUMAN], contract_cols, preferred_element_type=jnp.float32
            )

        def mouse_back(unused):
            return lax.dot_general(
                grad_mouse, piece[:, HUMAN:], contract_cols, preferred_element_type=jnp.float32
            )

        return lax.cond(is_human, human_back, mouse_back, 0)

    grad_out = back_piece(lax.all_gather(head_weight, "ch", axis=0, tiled=True))

    def human_term(unused):
        part = lax.dot_general(
            outputs, grad_human, contract_rows, preferred_element_type=jnp.float32
        )
        return jnp.concatenate(
            [
                part,
                jnp.zeros(
                    (lax.axis_size(("seq", "ch")) * (width // (seq_count * ch_count)), MOUSE),
                    jnp.float32,
                ),
            ],
            1,
        )

    def mouse_term(unused):
        part = lax.dot_general(
            outputs, grad_mouse, contract_rows, preferred_element_type=jnp.float32
        )
        return jnp.concatenate(
            [
                jnp.zeros(
                    (lax.axis_size(("seq", "ch")) * (width // (seq_count * ch_count)), HUMAN),
                    jnp.float32,
                ),
                part,
            ],
            1,
        )

    head_weight_grad = lax.psum_scatter(
        lax.cond(is_human, human_term, mouse_term, 0),
        ("seq", "ch"),
        scatter_dimension=0,
        tiled=True,
    )
    bias_part = jnp.concatenate(
        [jnp.sum(grad_human.astype(jnp.float32), 0), jnp.sum(grad_mouse.astype(jnp.float32), 0)]
    )
    grad_branch = grad_out.astype(jnp.bfloat16)
    mix_piece = lax.all_gather(grad_branch, "ch", axis=0, tiled=True)
    grad_rows = lax.dot_general(
        mix_piece, mix_weight, contract_cols, preferred_element_type=jnp.float32
    )
    grad_acts = grad_rows
    mix_part = lax.dot_general(
        act_two, mix_piece, contract_rows, preferred_element_type=jnp.float32
    )
    grad_pre_two = gelu_grad(pre_two, grad_acts)
    gain_part = jnp.sum(grad_pre_two * normed_two, 0)
    shift_part = jnp.sum(grad_pre_two, 0)
    gain_two_grad, shift_two_grad = lax.psum((gain_part, shift_part), "seq")
    convolution_gradient = (
        gain_two
        * scale_two
        * (grad_pre_two - shift_two_grad * inv_bins - normed_two * gain_two_grad * inv_bins)
    ).astype(jnp.bfloat16)
    padded_gradient = with_halo(convolution_gradient, (("seq", 0),), DILATION_STEP)
    conv_part = jnp.stack(
        [
            lax.dot_general(
                padded_input[
                    kernel_tap_index * DILATION_STEP : kernel_tap_index * DILATION_STEP
                    + residual_rows
                ],
                jnp.where(
                    fwd_masks[kernel_tap_index][:, None],
                    convolution_gradient,
                    jnp.zeros_like(convolution_gradient),
                ),
                contract_rows,
                preferred_element_type=jnp.float32,
            )
            for kernel_tap_index in range(TAPS)
        ]
    )
    total = jnp.zeros((lax.axis_size("ch") * local_rows, width), jnp.float32)
    for kernel_tap_index in range(TAPS):
        grad_rows = lax.dynamic_slice_in_dim(
            padded_gradient,
            (2 - kernel_tap_index) * DILATION_STEP,
            lax.axis_size("ch") * local_rows,
            0,
        )
        product = lax.dot_general(
            grad_rows,
            conv_weight[kernel_tap_index],
            contract_cols,
            preferred_element_type=jnp.float32,
        )
        total = total + product * back_masks[kernel_tap_index]
    grad_act_one = lax.psum_scatter(
        total.astype(jnp.bfloat16), "ch", scatter_dimension=0, tiled=True
    ).astype(jnp.float32)
    grad_pre_one = gelu_grad(pre_one, grad_act_one)
    gain_one_grad, shift_one_grad, head_bias_grad = lax.psum(
        (jnp.sum(grad_pre_one * normed_one, 0), jnp.sum(grad_pre_one, 0), bias_part), ("seq", "ch")
    )
    input_grad = grad_out + gain_one * scale_one * (
        grad_pre_one - shift_one_grad * inv_bins - normed_one * gain_one_grad * inv_bins
    )
    conv_weight_grad, mix_weight_grad = lax.psum((conv_part, mix_part), "seq")
    return (
        outputs,
        input_grad,
        gain_one_grad,
        shift_one_grad,
        conv_weight_grad,
        gain_two_grad,
        shift_two_grad,
        mix_weight_grad,
        head_weight_grad,
        head_bias_grad,
    )


def solution(mesh):
    in_specs = (
        P(("seq", "ch"), None),
        P(),
        P(),
        P(None, None, "ch"),
        P("ch"),
        P("ch"),
        P("ch", None),
        P("ch", None),
        P(),
        P(),
        P(("seq", "ch"), None),
    )
    out_specs = (
        P(("seq", "ch"), None),
        P(("seq", "ch"), None),
        P(),
        P(),
        P(None, None, "ch"),
        P("ch"),
        P("ch"),
        P("ch", None),
        P(("seq", "ch"), None),
        P(),
    )
    return jax.shard_map(
        on_device, mesh=mesh, in_specs=in_specs, out_specs=out_specs, check_vma=False
    )
```

profile of v0, /device:TPU:0, one launch (start us, length us, event | category | flops | bytes accessed | tf_op | source)
XLA Modules:
  0.0 632.3 jit_solution(14036912105792922197)
XLA Ops:
  8.4 42.1 %all-reduce.4 = (f32[768]{0:T(1024)S(1)}, f32[768]{0:T(1024)S(1)}) all-reduce(f32[768]{0:T(1024)S(1)} %get-tuple-element.95, f32[768]{0:T(1024)S(1)} %get-tuple-element.94), channel_id=1, replica_groups=mesh['seq'=8,'ch'=4] {'seq','ch'}, use_global_device_ids=true, to_apply=%region_3.0 | all-reduce | flops 1536 | bytes 12288 | tf_op jit(solution)/shard_map/psum | solution.py:71
  51.2 2.1 fusion.33
  53.5 19.5 %all-gather.4.cloned.1.call-done = bf16[1024,768]{1,0:T(8,128)(2,1)} async-done(((bf16[256,768]{1,0:T(8,128)(2,1)}), bf16[1024,768]{1,0:T(8,128)(2,1)}) %all-gather.4.cloned.1.call-update) | async-done | bytes 1572880 | tf_op jit(solution)/shard_map/all_gather | solution.py:79
  75.3 3.2 collective-permute-start.1
  80.6 2.0 convolution_select_fusion
  83.5 21.6 %all-reduce.6 = (f32[96]{0:T(128)S(1)}, f32[96]{0:T(128)S(1)}) all-reduce(f32[96]{0:T(128)S(1)} %get-tuple-element.93, f32[96]{0:T(128)S(1)} %get-tuple-element.92), channel_id=1, replica_groups=mesh['seq'=8,'ch'=4] {'seq'}, use_global_device_ids=true, to_apply=%region_7.8 | all-reduce | flops 192 | bytes 1536 | tf_op jit(solution)/shard_map/psum | solution.py:105
  109.2 6.2 copy.26
  115.5 5.3 convert_element_type.74
  120.8 10.7 %reduce-scatter.6.cloned.1.call-done = bf16[256,768]{1,0:T(8,128)(2,1)} async-done(((bf16[1024,768]{1,0:T(8,128)(2,1)}), bf16[256,768]{1,0:T(8,128)(2,1)}) %reduce-scatter.6.cloned.1.call-update) | async-done | bytes 393232 | tf_op jit(solution)/shard_map/reduce_scatter | solution.py:111
  133.3 71.9 %all-gather.6.cloned.1.call-done = bf16[768,6956]{1,0:T(8,128)(2,1)} async-done(((bf16[192,6956]{1,0:T(8,128)(2,1)}), bf16[768,6956]{1,0:T(8,128)(2,1)}) %all-gather.6.cloned.1.call-update) | async-done | bytes 10684432 | tf_op jit(solution)/shard_map/all_gather | solution.py:168
  205.3 4.7 conditional.4
  205.3 4.4 fusion
  210.0 7.2 %conditional.5 = (bf16[256,5313]{1,0:T(8,128)(2,1)S(1)}, bf16[256,1643]{1,0:T(8,128)(2,1)}) conditional(s32[]{:T(128)} %convert_element_type.73, (f32[6956]{0:T(1024)S(1)}, f32[256,1643]{0,1:T(8,128)S(1)}, f32[256,5313]{1,0:T(8,128)}) %tuple.87, (f32[6956]{0:T(1024)S(1)}, f32[256,5313]{1,0:T(8,128)S(1)}, f32[256,5313]{1,0:T(8,128)}) %tuple.88), branch_computations={%region_12.13_spmd, %region_13.14_spmd} | conditional | flops 19041792 | bytes 17040690 | solution.py:152
  213.2 3.8 fusion.7
  217.2 4.1 conditional.6
  217.2 4.1 fusion.12
  223.4 23.7 %all-gather.8.cloned.1.call-done = bf16[1024,768]{1,0:T(8,128)(2,1)} async-done(((bf16[256,768]{1,0:T(8,128)(2,1)}), bf16[1024,768]{1,0:T(8,128)(2,1)}) %all-gather.8.cloned.1.call-update) | async-done | bytes 1572880 | tf_op jit(solution)/shard_map/all_gather | solution.py:210
  247.1 3.0 fusion.96
  250.1 21.4 %all-reduce.5 = (f32[96]{0:T(128)S(1)}, f32[96]{0:T(128)S(1)}) all-reduce(f32[96]{0:T(128)S(1)} %get-tuple-element.91, f32[96]{0:T(128)S(1)} %get-tuple-element.90), channel_id=1, replica_groups=mesh['seq'=8,'ch'=4] {'seq'}, use_global_device_ids=true, to_apply=%region_19.20 | all-reduce | flops 192 | bytes 1536 | tf_op jit(solution)/shard_map/psum | solution.py:221
  274.5 2.1 collective-permute-start.3
  277.6 3.5 collective-permute-done.3
  281.1 2.2 add_convert_fusion
  283.6 2.1 convolution_bitcast_fusion.2
  289.0 13.7 %conditional.7 = (f32[768,6956]{0,1:T(8,128)}) conditional(s32[]{:T(128)} %convert_element_type.73, (bf16[256,768]{1,0:T(8,128)(2,1)}, bf16[256,1643]{1,0:T(8,128)(2,1)}) %tuple.41, (bf16[256,768]{1,0:T(8,128)(2,1)}, bf16[256,5313]{1,0:T(8,128)(2,1)S(1)}) %tuple.42), branch_computations={%region_27.28_spmd, %region_28.29_spmd} | conditional | flops 2089156608 | bytes 57125388 | solution.py:201
  289.0 2.2 fusion.102
  291.2 11.5 %concatenate.16 = f32[768,6956]{0,1:T(8,128)} pad(f32[768,1643]{0,1:T(8,128)S(1)} %fusion.102, f32[]{:T(128)} %constant.156.clone), padding=0_0x5313_0 | pad | bytes 26416132 | tf_op jit(solution)/shard_map/cond/branch_0_fun/concatenate | solution.py:189
  302.7 21.4 %copy.28 = f32[768,6956]{1,0:T(8,128)} copy(f32[768,6956]{0,1:T(8,128)} %get-tuple-element.145) | data formatting | bytes 42737664 | tf_op jit(solution)/shard_map/cond | solution.py:201
  327.8 37.9 %all-reduce.3 = (f32[768]{0:T(1024)S(1)}, f32[768]{0:T(1024)S(1)}, f32[6956]{0:T(1024)}) all-reduce(f32[768]{0:T(1024)S(1)} %get-tuple-element.89, f32[768]{0:T(1024)S(1)} %get-tuple-element.88, f32[6956]{0:T(1024)S(1)} %pad_maximum_fusion.11), channel_id=1, replica_groups=mesh['seq'=8,'ch'=4] {'seq','ch'}, use_global_device_ids=true, to_apply=%region_24.25 | all-reduce | flops 8492 | bytes 67936 | tf_op jit(solution)/shard_map/psum | solution.py:265
  365.8 2.2 fusion.38
  368.0 24.2 %all-reduce.10.cloned.1.call-done = (f32[3,768,96]{1,2,0:T(8,128)}, f32[96,768]{1,0:T(8,128)}) async-done(((f32[3,768,96]{1,2,0:T(8,128)}, f32[96,768]{1,0:T(8,128)}), (f32[3,768,96]{1,2,0:T(8,128)}, f32[96,768]{1,0:T(8,128)})) %all-reduce.10.cloned.1.call-update) | async-done | bytes 1179664 | tf_op jit(solution)/shard_map/psum | solution.py:271
  392.2 229.4 %reduce-scatter.10.cloned.1.call-done = f32[24,6956]{1,0:T(8,128)} async-done(((f32[768,6956]{1,0:T(8,128)}), f32[24,6956]{1,0:T(8,128)}) %reduce-scatter.10.cloned.1.call-update) | async-done | bytes 667792
  621.6 2.1 copy.44
  (101 shorter events, 30.8 us)
Async XLA Ops:
  7.2 97.9 %copy-start = (bf16[96,768]{1,0:T(8,128)(2,1)S(1)}, bf16[96,768]{1,0:T(8,128)(2,1)}, u32[]{:S(2)}) copy-start(bf16[96,768]{1,0:T(8,128)(2,1)} %param.25) | copy-start | bytes 442372
  7.2 73.4 %copy-start.8 = (bf16[3,768,96]{1,2,0:T(8,128)(2,1)S(1)}, bf16[3,768,96]{1,2,0:T(8,128)(2,1)}, u32[]{:S(2)}) copy-start(bf16[3,768,96]{1,2,0:T(8,128)(2,1)} %param.22) | copy-start | bytes 1327108
  7.2 65.8 %all-gather.4.cloned.1.call-start = ((), (), s32[]{:S(2)}) async-start(), calls=%async_computation.3 | async-start | bytes 1966080 | tf_op jit(solution)/shard_map/all_gather | solution.py:79
  53.4 78.1 %reduce-scatter.6.cloned.1.call-start = ((), (), s32[]{:S(2)}) async-start(), calls=%async_computation.4 | async-start | bytes 1966080 | tf_op jit(solution)/shard_map/reduce_scatter | solution.py:111
  73.8 8.9 %collective-permute-start = (bf16[11,768]{1,0:T(8,128)(2,1)S(1)}, bf16[11,768]{1,0:T(8,128)(2,1)S(1)}, u32[]{:S(2)}, u32[]{:S(2)}) collective-permute-start(bf16[11,768]{1,0:T(8,128)(2,1)S(1)} %get-tuple-element.109), channel_id=1, source_target_pairs={{0,4},{4,8},{8,12},{12,16},{16,20},{20,24},{24,28},{28,0},{1,5},{5... | collective-permute-start | bytes 50696 | tf_op jit(solution)/shard_map/ppermute | solution.py:24
  75.3 7.4 %copy-start.4 = (bf16[1024,768]{1,0:T(8,128)(2,1)S(1)}, bf16[1024,768]{1,0:T(8,128)(2,1)}, u32[]{:S(2)}) copy-start(bf16[1024,768]{1,0:T(8,128)(2,1)} %all-gather.4.cloned.1.call-done) | copy-start | bytes 4718596
  75.3 5.3 collective-permute-start.1
  80.6 2.8 copy-start.21
  82.7 22.4 %copy-start.15 = (f32[96]{0:T(128)S(1)}, f32[96]{0:T(128)}, u32[]{:S(2)}) copy-start(f32[96]{0:T(128)} %param.23) | copy-start | bytes 1156
  82.7 22.4 %copy-start.17 = (f32[96]{0:T(128)S(1)}, f32[96]{0:T(128)}, u32[]{:S(2)}) copy-start(f32[96]{0:T(128)} %param.24) | copy-start | bytes 1156
  82.7 24.4 %copy-start.19 = (bf16[11,768]{1,0:T(8,128)(2,1)}, bf16[11,768]{1,0:T(8,128)(2,1)S(1)}, u32[]{:S(2)}) copy-start(bf16[11,768]{1,0:T(8,128)(2,1)S(1)} %collective-permute-done) | copy-start | bytes 50692
  83.5 24.4 %copy-start.6 = (f32[1024,96]{0,1:T(8,128)}, f32[1024,96]{0,1:T(8,128)S(1)}, u32[]{:S(2)}) copy-start(f32[1024,96]{0,1:T(8,128)S(1)} %get-tuple-element.119) | copy-start | bytes 1179652
  105.1 2.8 copy-start.23
  107.1 98.2 %all-gather.6.cloned.1.call-start = ((), (), s32[]{:S(2)}) async-start(), calls=%async_computation.5 | async-start | bytes 13516800 | tf_op jit(solution)/shard_map/all_gather | solution.py:168
  107.8 139.3 %all-gather.8.cloned.1.call-start = ((), (), s32[]{:S(2)}) async-start(), calls=%async_computation.6 | async-start | bytes 1966080 | tf_op jit(solution)/shard_map/all_gather | solution.py:210
  115.5 16.0 %copy-start.2 = (bf16[256,768]{1,0:T(8,128)(2,1)S(1)}, bf16[256,768]{1,0:T(8,128)(2,1)}, u32[]{:S(2)}) copy-start(bf16[256,768]{1,0:T(8,128)(2,1)} %param.19) | copy-start | bytes 1179652
  205.3 4.7 copy-start.10
  223.3 102.7 %reduce-scatter.8.cloned.1.call-start = ((), (), s32[]{:S(2)}) async-start(), calls=%async_computation.7 | async-start | bytes 1966080 | tf_op jit(solution)/shard_map/reduce_scatter | solution.py:261
  271.5 6.1 copy-start.16
  271.5 6.1 copy-start.24
  271.5 5.3 copy-start.9
  273.0 3.9 collective-permute-start.2
  274.5 6.6 %collective-permute-start.3 = (bf16[11,96]{0,1:T(8,128)(2,1)S(1)}, bf16[11,96]{0,1:T(8,128)(2,1)S(1)}, u32[]{:S(2)}, u32[]{:S(2)}) collective-permute-start(bf16[11,96]{0,1:T(8,128)(2,1)S(1)} %get-tuple-element.111), channel_id=1, source_target_pairs={{0,4},{4,8},{8,12},{12,16},{16,20},{20,24},{24,28},{28,0},{1,5},{5... | collective-permute-start | bytes 6344 | tf_op jit(solution)/shard_map/ppermute | solution.py:24
  281.1 2.5 copy-start.20
  283.3 2.4 copy-start.22
  283.3 108.9 %all-reduce.10.cloned.1.call-start = ((), (), s32[]{:S(2)}) async-start(), calls=%async_computation.9 | async-start | bytes 2359296 | tf_op jit(solution)/shard_map/psum | solution.py:271
  283.6 2.1 copy-start.5
  285.7 2.0 copy-start.7
  289.0 332.7 %reduce-scatter.10.cloned.1.call-start = ((), (), s32[]{:S(2)}) async-start(), calls=%async_computation.8 | async-start | bytes 22302720
  326.0 299.4 %copy-start.1 = (bf16[96,768]{1,0:T(8,128)(2,1)S(1)}, bf16[96,768]{1,0:T(8,128)(2,1)}, u32[]{:S(2)}) copy-start(bf16[96,768]{1,0:T(8,128)(2,1)} %param.25) | copy-start | bytes 442372
  365.8 259.7 %copy-start.13 = (f32[768]{0:T(1024)}, f32[768]{0:T(1024)S(1)}, u32[]{:S(2)}) copy-start(f32[768]{0:T(1024)S(1)} %get-tuple-element.134) | copy-start | bytes 9220
  365.8 259.7 %copy-start.14 = (f32[768]{0:T(1024)}, f32[768]{0:T(1024)S(1)}, u32[]{:S(2)}) copy-start(f32[768]{0:T(1024)S(1)} %get-tuple-element.135) | copy-start | bytes 9220
  (4 other events, 6.9 us)
Sparse Core Ops, SparseCore 0:
  53.5 19.4 all-gather.3
  107.2 24.2 reduce-scatter.5
  133.1 72.0 all-gather.5
  223.4 23.6 all-gather.7
  283.4 24.4 reduce-scatter.7
  311.9 80.2 all-reduce.9
  400.4 221.2 reduce-scatter.9
where the time goes:
time: 634 us; the launch traced here: 632 us
  waiting for transfers between devices  384 us (61%)
  blocking collectives  123 us (19%)
  local copies, waits for them, and re-layouts  47.5 us (7%)
  matrix products  29.1 us (5%)
  other arithmetic  25.8 us (4%)
  between operations  15.2 us (2%)
  starting transfers between devices  7.34 us (1%)
    unnamed x8, waiting for transfers between devices  230 us
    all_gather x1, waiting for transfers between devices, on_device(): grad_out = back_piece(lax.all_gather(head_weight, 'ch', axis=0, tiled=True))  71.9 us
    psum x1, blocking collectives, on_device(): lax.psum((jnp.sum(input_f, 0), jnp.sum(input_f * input_f, 0)), ('seq', 'c...  42.1 us
    psum x1, blocking collectives, on_device(): lax.psum((jnp.sum(grad_pre_one * normed_one, 0), jnp.sum(grad_pre_one, 0)...  37.9 us
    psum x1, waiting for transfers between devices, on_device(): conv_weight_grad, mix_weight_grad = lax.psum((conv_part, mix_part), 'seq')  24.2 us
    all_gather x1, waiting for transfers between devices, on_device(): mix_piece = lax.all_gather(grad_branch, 'ch', axis=0, tiled=True)  23.7 us
    psum x1, blocking collectives, on_device(): lax.psum((jnp.sum(conv_out, 0), jnp.sum(conv_out * conv_out, 0)), 'seq')  21.6 us
    cond x1, local copies, waits for them, and re-layouts, on_device(): lax.cond(is_human, human_term, mouse_term, 0)  21.4 us
  transfers between devices with their start and end apart: 11, of which 8 were waited for; matrix products, arithmetic and copies ran while one was open for 11% of the time, Pallas kernels for 0%

commit v1 on v0

--- a/solution.py
+++ b/solution.py
@@ -12,6 +12,18 @@
 norm_eps = 1e-05
 contract_rows = (((0,), (0,)), ((), ()))
 contract_cols = (((1,), (1,)), ((), ()))
+
+
+def collect(x, axis, dim):
+    ways, here = (lax.axis_size(axis), lax.axis_index(axis))
+    grown, reach = (x, 1)
+    while reach < ways:
+        theirs = lax.ppermute(grown, axis, [(d, d ^ reach) for d in range(ways)])
+        mine_first = jnp.concatenate([grown, theirs], axis=dim)
+        theirs_first = jnp.concatenate([theirs, grown], axis=dim)
+        grown = jnp.where(here & reach == 0, mine_first, theirs_first)
+        reach = 2 * reach
+    return grown
 
 
 def with_halo(cells, sides, width):
@@ -165,7 +177,7 @@
 
         return lax.cond(is_human, human_back, mouse_back, 0)
 
-    grad_out = back_piece(lax.all_gather(head_weight, "ch", axis=0, tiled=True))
+    grad_out = back_piece(collect(head_weight, "ch", 0))
 
     def human_term(unused):
         part = lax.dot_general(

time: 634 us -> 754 us (1.19)
  waiting for transfers between devices: 384 us -> 466 us
  other arithmetic: 25.8 us -> 45.3 us
  local copies, waits for them, and re-layouts: 47.5 us -> 64.8 us
    ppermute x0 -> x2, waiting for transfers between devices: none -> 167 us  [collect(): theirs = lax.ppermute(grown, axis, [(d, d ^ reach) for d in range(ways)])]
    all_gather x1, waiting for transfers between devices: 71.9 us -> 0.01 us  [on_device(): piece = lax.all_gather(head_weight, 'ch', axis=0, tiled=True)]
    select_n x0 -> x2, other arithmetic: none -> 21.2 us  [collect(): grown = jnp.where(here & reach == 0, mine_first, theirs_first)]
    reduce_scatter x1, waiting for transfers between devices: 10.7 us -> 0.01 us  [on_device(): lax.psum_scatter(jnp.dot(act_two, mix_weight, preferred_element_type=jnp....]
    select_n x0 -> x1, local copies, waits for them, and re-layouts: none -> 8.2 us  [collect(): grown = jnp.where(here & reach == 0, mine_first, theirs_first)]
    ppermute x0 -> x1, local copies, waits for them, and re-layouts: none -> 8.07 us  [collect(): theirs = lax.ppermute(grown, axis, [(d, d ^ reach) for d in range(ways)])]
  transfers between devices with their start and end apart: 11 -> 13, of which waited for: 8 -> 8; matrix products, arithmetic and copies ran while one was open for 11% -> 14% of each run, Pallas kernels for 0% -> 0%
where the time goes in v1:
time: 754 us; the launch traced here: 753 us
  waiting for transfers between devices  466 us (62%)
  blocking collectives  123 us (16%)
  local copies, waits for them, and re-layouts  64.8 us (9%)
  other arithmetic  45.3 us (6%)
  matrix products  30.3 us (4%)
  between operations  15.2 us (2%)
  starting transfers between devices  7.6 us (1%)
    unnamed x8, waiting for transfers between devices  230 us
    ppermute x2, waiting for transfers between devices, collect(): theirs = lax.ppermute(grown, axis, [(d, d ^ reach) for d in range(ways)])  167 us
    psum x1, blocking collectives, on_device(): lax.psum((jnp.sum(input_f, 0), jnp.sum(input_f * input_f, 0)), ('seq', 'c...  42.1 us
    psum x1, blocking collectives, on_device(): lax.psum((jnp.sum(grad_pre_one * normed_one, 0), jnp.sum(grad_pre_one, 0)...  37.9 us
    psum x1, waiting for transfers between devices, on_device(): conv_weight_grad, mix_weight_grad = lax.psum((conv_part, mix_part), 'seq')  23.1 us
    all_gather x1, waiting for transfers between devices, on_device(): mix_piece = lax.all_gather(grad_branch, 'ch', axis=0, tiled=True)  22.7 us
    psum x1, blocking collectives, on_device(): lax.psum((jnp.sum(conv_out, 0), jnp.sum(conv_out * conv_out, 0)), 'seq')  21.6 us
    cond x1, local copies, waits for them, and re-layouts, on_device(): lax.cond(is_human, human_term, mouse_term, 0)  21.4 us
  transfers between devices with their start and end apart: 13, of which 8 were waited for; matrix products, arithmetic and copies ran while one was open for 14% of the time, Pallas kernels for 0%

profile of v1, /device:TPU:0, one launch (start us, length us, event | category | flops | bytes accessed | tf_op | source)
XLA Modules:
  0.0 752.6 jit_solution(9828747990214502687)
XLA Ops:
  8.4 42.1 %all-reduce.4 = (f32[768]{0:T(1024)S(1)}, f32[768]{0:T(1024)S(1)}) all-reduce(f32[768]{0:T(1024)S(1)} %get-tuple-element.104, f32[768]{0:T(1024)S(1)} %get-tuple-element.103), channel_id=1, replica_groups=mesh['seq'=8,'ch'=4] {'seq','ch'}, use_global_device_ids=true, to_apply=%region_3.0 | all-reduce | flops 1536 | bytes 12288 | tf_op jit(solution)/shard_map/psum | solution.py:83
  53.5 19.5 %all-gather.4.cloned.1.call-done = bf16[1024,768]{1,0:T(8,128)(2,1)} async-done(((bf16[256,768]{1,0:T(8,128)(2,1)}), bf16[1024,768]{1,0:T(8,128)(2,1)}) %all-gather.4.cloned.1.call-update) | async-done | bytes 1572880 | tf_op jit(solution)/shard_map/all_gather | solution.py:91
  75.4 3.2 collective-permute-start.1
  83.6 21.6 %all-reduce.6 = (f32[96]{0:T(128)S(1)}, f32[96]{0:T(128)S(1)}) all-reduce(f32[96]{0:T(128)S(1)} %get-tuple-element.102, f32[96]{0:T(128)S(1)} %get-tuple-element.101), channel_id=1, replica_groups=mesh['seq'=8,'ch'=4] {'seq'}, use_global_device_ids=true, to_apply=%region_7.8 | all-reduce | flops 192 | bytes 1536 | tf_op jit(solution)/shard_map/psum | solution.py:117
  108.1 5.4 collective-permute-done.2
  113.5 7.2 maximum_select_fusion.1
  120.6 8.2 %copy.35 = bf16[384,6956]{0,1:T(8,128)(2,1)} copy(bf16[384,6956]{1,0:T(8,128)(2,1)} %maximum_select_fusion.1) | data formatting | bytes 10684416 | tf_op jit(solution)/shard_map/jit(_where)/select_n | solution.py:24
  130.3 6.1 copy.38
  136.4 5.3 convert_element_type.74
  142.8 161.6 %collective-permute-done.3 = bf16[384,6956]{0,1:T(8,128)(2,1)} collective-permute-done((bf16[384,6956]{0,1:T(8,128)(2,1)}, bf16[384,6956]{0,1:T(8,128)(2,1)}, u32[]{:S(2)}, u32[]{:S(2)}) %collective-permute-start.3) | collective-permute-done | bytes 5342240 | tf_op jit(solution)/shard_map/ppermute | solution.py:21
  304.4 8.1 %copy.36 = bf16[384,6956]{1,0:T(8,128)(2,1)} copy(bf16[384,6956]{0,1:T(8,128)(2,1)} %collective-permute-done.3) | data formatting | bytes 10684416 | tf_op jit(solution)/shard_map/ppermute | solution.py:21
  312.5 14.1 %maximum_select_fusion = bf16[768,6956]{1,0:T(8,128)(2,1)} fusion(bf16[384,6956]{1,0:T(8,128)(2,1)} %copy.36, bf16[384,6956]{1,0:T(8,128)(2,1)} %maximum_select_fusion.1, pred[]{:T(512)S(6)} %eq.54), kind=kLoop, calls=%fused_computation.18 | loop fusion | flops 48079872 | bytes 21368832 | tf_op jit(solution)/shard_map/jit(_where)/select_n | solution.py:24
  326.6 4.8 conditional.4
  326.6 4.2 fusion
  331.4 6.1 conditional.5
  334.4 2.9 fusion.7
  338.4 3.9 conditional.6
  338.4 3.9 fusion.12
  344.3 22.7 %all-gather.8.cloned.1.call-done = bf16[1024,768]{1,0:T(8,128)(2,1)} async-done(((bf16[256,768]{1,0:T(8,128)(2,1)}), bf16[1024,768]{1,0:T(8,128)(2,1)}) %all-gather.8.cloned.1.call-update) | async-done | bytes 1572880 | tf_op jit(solution)/shard_map/all_gather | solution.py:222
  367.0 3.0 fusion.96
  370.0 21.4 %all-reduce.5 = (f32[96]{0:T(128)S(1)}, f32[96]{0:T(128)S(1)}) all-reduce(f32[96]{0:T(128)S(1)} %get-tuple-element.100, f32[96]{0:T(128)S(1)} %get-tuple-element.99), channel_id=1, replica_groups=mesh['seq'=8,'ch'=4] {'seq'}, use_global_device_ids=true, to_apply=%region_19.20 | all-reduce | flops 192 | bytes 1536 | tf_op jit(solution)/shard_map/psum | solution.py:233
  394.4 2.3 collective-permute-start.5
  397.7 3.5 collective-permute-done.5
  401.2 2.2 add_convert_fusion
  405.6 2.2 convolution_bitcast_fusion
  410.5 13.8 %conditional.7 = (f32[768,6956]{0,1:T(8,128)}) conditional(s32[]{:T(128)} %convert_element_type.73, (bf16[256,768]{1,0:T(8,128)(2,1)}, bf16[256,1643]{1,0:T(8,128)(2,1)}) %tuple.92, (bf16[256,768]{1,0:T(8,128)(2,1)}, bf16[256,5313]{1,0:T(8,128)(2,1)S(1)}) %tuple.93), branch_computations={%region_27.28_spmd, %region_28.29_spmd} | conditional | flops 2089156608 | bytes 57125388 | solution.py:213
  412.6 11.6 %concatenate.24 = f32[768,6956]{0,1:T(8,128)} pad(f32[768,1643]{0,1:T(8,128)S(1)} %fusion.102, f32[]{:T(128)} %constant.158.clone), padding=0_0x5313_0 | pad | bytes 26416132 | tf_op jit(solution)/shard_map/cond/branch_0_fun/concatenate | solution.py:201
  424.3 21.4 %copy.40 = f32[768,6956]{1,0:T(8,128)} copy(f32[768,6956]{0,1:T(8,128)} %get-tuple-element.154) | data formatting | bytes 42737664 | tf_op jit(solution)/shard_map/cond | solution.py:213
  449.3 37.9 %all-reduce.3 = (f32[768]{0:T(1024)S(1)}, f32[768]{0:T(1024)S(1)}, f32[6956]{0:T(1024)}) all-reduce(f32[768]{0:T(1024)S(1)} %get-tuple-element.98, f32[768]{0:T(1024)S(1)} %get-tuple-element.97, f32[6956]{0:T(1024)S(1)} %pad_maximum_fusion.11), channel_id=1, replica_groups=mesh['seq'=8,'ch'=4] {'seq','ch'}, use_global_device_ids=true, to_apply=%region_24.25 | all-reduce | flops 8492 | bytes 67936 | tf_op jit(solution)/shard_map/psum | solution.py:277
  487.2 2.3 fusion.38
  489.4 23.1 %all-reduce.10.cloned.1.call-done = (f32[3,768,96]{1,2,0:T(8,128)}, f32[96,768]{1,0:T(8,128)}) async-done(((f32[3,768,96]{1,2,0:T(8,128)}, f32[96,768]{1,0:T(8,128)}), (f32[3,768,96]{1,2,0:T(8,128)}, f32[96,768]{1,0:T(8,128)})) %all-reduce.10.cloned.1.call-update) | async-done | bytes 1179664 | tf_op jit(solution)/shard_map/psum | solution.py:283
  512.5 229.4 %reduce-scatter.10.cloned.1.call-done = f32[24,6956]{1,0:T(8,128)} async-done(((f32[768,6956]{1,0:T(8,128)}), f32[24,6956]{1,0:T(8,128)}) %reduce-scatter.10.cloned.1.call-update) | async-done | bytes 667792
  (115 shorter events, 41.0 us)
Async XLA Ops:
  7.2 98.0 %copy-start = (bf16[96,768]{1,0:T(8,128)(2,1)S(1)}, bf16[96,768]{1,0:T(8,128)(2,1)}, u32[]{:S(2)}) copy-start(bf16[96,768]{1,0:T(8,128)(2,1)} %param.25) | copy-start | bytes 442372
  7.2 73.5 %copy-start.11 = (bf16[3,768,96]{1,2,0:T(8,128)(2,1)S(1)}, bf16[3,768,96]{1,2,0:T(8,128)(2,1)}, u32[]{:S(2)}) copy-start(bf16[3,768,96]{1,2,0:T(8,128)(2,1)} %param.22) | copy-start | bytes 1327108
  7.2 65.8 %all-gather.4.cloned.1.call-start = ((), (), s32[]{:S(2)}) async-start(), calls=%async_computation.3 | async-start | bytes 1966080 | tf_op jit(solution)/shard_map/all_gather | solution.py:91
  53.4 88.3 %reduce-scatter.6.cloned.1.call-start = ((), (), s32[]{:S(2)}) async-start(), calls=%async_computation.4 | async-start | bytes 1966080 | tf_op jit(solution)/shard_map/reduce_scatter | solution.py:123
  73.0 9.8 %copy-start.7 = (bf16[1024,768]{1,0:T(8,128)(2,1)S(1)}, bf16[1024,768]{1,0:T(8,128)(2,1)}, u32[]{:S(2)}) copy-start(bf16[1024,768]{1,0:T(8,128)(2,1)} %all-gather.4.cloned.1.call-done) | copy-start | bytes 4718596
  73.9 8.9 %collective-permute-start = (bf16[11,768]{1,0:T(8,128)(2,1)S(1)}, bf16[11,768]{1,0:T(8,128)(2,1)S(1)}, u32[]{:S(2)}, u32[]{:S(2)}) collective-permute-start(bf16[11,768]{1,0:T(8,128)(2,1)S(1)} %get-tuple-element.118), channel_id=1, source_target_pairs={{0,4},{4,8},{8,12},{12,16},{16,20},{20,24},{24,28},{28,0},{1,5},{5... | collective-permute-start | bytes 50696 | tf_op jit(solution)/shard_map/ppermute | solution.py:36
  75.4 5.3 collective-permute-start.1
  80.7 24.4 %copy-start.18 = (f32[96]{0:T(128)S(1)}, f32[96]{0:T(128)}, u32[]{:S(2)}) copy-start(f32[96]{0:T(128)} %param.23) | copy-start | bytes 1156
  80.8 24.5 %copy-start.20 = (f32[96]{0:T(128)S(1)}, f32[96]{0:T(128)}, u32[]{:S(2)}) copy-start(f32[96]{0:T(128)} %param.24) | copy-start | bytes 1156
  82.8 24.4 %copy-start.22 = (bf16[11,768]{1,0:T(8,128)(2,1)}, bf16[11,768]{1,0:T(8,128)(2,1)S(1)}, u32[]{:S(2)}) copy-start(bf16[11,768]{1,0:T(8,128)(2,1)S(1)} %collective-permute-done) | copy-start | bytes 50692
  83.6 24.4 %copy-start.9 = (f32[1024,96]{0,1:T(8,128)}, f32[1024,96]{0,1:T(8,128)S(1)}, u32[]{:S(2)}) copy-start(f32[1024,96]{0,1:T(8,128)S(1)} %get-tuple-element.128) | copy-start | bytes 1179652
  107.2 219.4 %all-gather.6.cloned.1.call-start = ((), (), s32[]{:S(2)}) async-start(), calls=%async_computation.5 | async-start | bytes 13516800 | tf_op jit(solution)/shard_map/all_gather | solution.py:142
  108.0 259.0 %all-gather.8.cloned.1.call-start = ((), (), s32[]{:S(2)}) async-start(), calls=%async_computation.6 | async-start | bytes 1966080 | tf_op jit(solution)/shard_map/all_gather | solution.py:222
  108.0 5.5 collective-permute-start.2
  120.6 8.4 %copy-start.26 = (s32[8]{0:T(128)S(1)}, s32[8]{0:T(128)}, u32[]{:S(2)}) copy-start(s32[8]{0:T(128)} %param.28) | copy-start | bytes 100
  128.8 175.6 %collective-permute-start.3 = (bf16[384,6956]{0,1:T(8,128)(2,1)}, bf16[384,6956]{0,1:T(8,128)(2,1)}, u32[]{:S(2)}, u32[]{:S(2)}) collective-permute-start(bf16[384,6956]{0,1:T(8,128)(2,1)} %copy.35), channel_id=1, source_target_pairs={{0,2},{1,3},{2,0},{3,1},{4,6},{5,7},{6,4},{7,5},{8,10},{9,11},{10,... | collective-permute-start | bytes 16026632 | tf_op jit(solution)/shard_map/ppermute | solution.py:21
  136.4 5.3 copy-start.3
  142.8 183.7 %copy-start.5 = (bf16[256,768]{1,0:T(8,128)(2,1)}, bf16[256,768]{1,0:T(8,128)(2,1)S(1)}, u32[]{:S(2)}) copy-start(bf16[256,768]{1,0:T(8,128)(2,1)S(1)} %fusion.40) | copy-start | bytes 1179652
  326.6 4.8 copy-start.13
  344.2 103.3 %reduce-scatter.8.cloned.1.call-start = ((), (), s32[]{:S(2)}) async-start(), calls=%async_computation.7 | async-start | bytes 1966080 | tf_op jit(solution)/shard_map/reduce_scatter | solution.py:273
  391.4 6.3 copy-start.19
  391.4 6.3 copy-start.27
  391.4 5.6 copy-start.12
  392.9 4.1 collective-permute-start.4
  394.4 6.8 collective-permute-start.5
  403.4 109.1 %all-reduce.10.cloned.1.call-start = ((), (), s32[]{:S(2)}) async-start(), calls=%async_computation.9 | async-start | bytes 2359296 | tf_op jit(solution)/shard_map/psum | solution.py:283
  403.5 4.3 copy-start.8
  405.6 3.6 copy-start.10
  410.4 331.5 %reduce-scatter.10.cloned.1.call-start = ((), (), s32[]{:S(2)}) async-start(), calls=%async_computation.8 | async-start | bytes 22302720
  447.5 298.3 %copy-start.1 = (bf16[96,768]{1,0:T(8,128)(2,1)S(1)}, bf16[96,768]{1,0:T(8,128)(2,1)}, u32[]{:S(2)}) copy-start(bf16[96,768]{1,0:T(8,128)(2,1)} %param.25) | copy-start | bytes 442372
  487.2 258.6 %copy-start.16 = (f32[768]{0:T(1024)}, f32[768]{0:T(1024)S(1)}, u32[]{:S(2)}) copy-start(f32[768]{0:T(1024)S(1)} %get-tuple-element.143) | copy-start | bytes 9220
  487.2 258.6 %copy-start.17 = (f32[768]{0:T(1024)}, f32[768]{0:T(1024)S(1)}, u32[]{:S(2)}) copy-start(f32[768]{0:T(1024)S(1)} %get-tuple-element.144) | copy-start | bytes 9220
  (9 other events, 19.5 us)
Sparse Core Ops, SparseCore 0:
  53.5 19.4 all-gather.3
  107.3 24.2 reduce-scatter.5
  133.2 134.4 all-gather.5
  344.3 22.6 all-gather.7
  403.5 24.4 reduce-scatter.7
  432.0 80.5 all-reduce.9
  520.7 221.2 reduce-scatter.9
